TPU v7x, 32 devices: a whole 2x2x4 slice. The times are simulated.
32 devices in a mesh: seed: 4 (over x, core), train: 8 (over z, y).
Axes of the slice: x: 2, y: 2, z: 4, core: 2. Of those that a mesh axis runs over, the one named last changes fastest.
Arguments:
- coordinates: float32 [16, 524288], P('seed', 'train'), parts along dimension 0, may hold values from -6 to 6
- slice_index: int32 [2097152], P(('seed', 'train')), parts along dimension 0, may hold values from 0 to 127, as said below
- history: float32 [32, 2, 128, 1024], P('seed', None, None, 'train'), parts along dimension 0, may hold values from -3 to 3
- impedance: float32 [9, 2, 1024], replicated, may hold values from -1.2 to 1.2
- slice_wake: float32 [128, 128], replicated, may hold values from -0.5 to 0.5
- tunes: float32 [8], P('seed'), parts along dimension 0, may hold values from 0.05 to 0.45
- detuning: float32 [8], P('seed'), parts along dimension 0, may hold values from 0.1 to 0.4
Outputs:
- tracked: float32 [16, 524288], P('seed', 'train'), parts along dimension 0
- moments: float32 [8, 128, 1024], P('seed', None, 'train'), parts along dimension 0
There are 4 independent parts, one for each index of `seed`. A program takes and returns all parts, laid end to end along the dimension named above; an argument that names none is the same for every part. Nothing has to cross between parts.
Inputs may be any that keep to these rules, and one draw needn't show every extreme that they name: `slice_index`: within each bunch, that is each aligned block of 512 entries, every slice number appears exactly 512 // 128 times.
All inputs are finite; a program needn't handle non-finite values.
Results may differ from a plain program's by a relative error of at most 0.00005.
Values sent between devices are 32-bit elements; how exact they have to be, the bound alone decides.
No kernel may reach another device: no remote copies, remote signals or barrier semaphores. Data moves between devices by JAX's collectives and lax.ppermute only.
A program may use at most 64 MiB of HBM per device.

v0:
```python
import math
import jax
import jax.numpy as jnp
from jax import lax
from jax.sharding import PartitionSpec as P

full_turn = 2.0 * math.pi


def rotate(positions, pushes, tunes, detuning):
    result = []
    for plane_index in range(2):
        position = positions[2 * plane_index]
        slope = positions[2 * plane_index + 1] + pushes[plane_index]
        action = 0.5 * (position * position + slope * slope)
        phase = full_turn * tunes[plane_index] + detuning[plane_index] * action
        cosine = jnp.cos(phase)
        sine = jnp.sin(phase)
        result.append(cosine * position + sine * slope)
        result.append(cosine * slope - sine * position)
    return jnp.stack(result)


def phase_tables(row_count, col_count, period):
    first = lax.broadcasted_iota(jnp.int32, (row_count, col_count), 0)
    second = lax.broadcasted_iota(jnp.int32, (row_count, col_count), 1)
    angle = full_turn / period * (first * second % period).astype(jnp.float32)
    return (jnp.cos(angle), jnp.sin(angle))


def contract(form, table, values):
    return jnp.einsum(form, table, values, precision=lax.Precision.HIGHEST)


def forward(series):
    item_count, column_count, bunch_total = series.shape
    trains = lax.axis_size("train")
    bunch_dev = bunch_total // trains
    signal = series.reshape(item_count, column_count, trains, bunch_dev)
    cos_train, sin_train = phase_tables(trains, trains, trains)
    first_re = contract("kp,ncpj->nckj", cos_train, signal)
    first_im = -contract("kp,ncpj->nckj", sin_train, signal)
    cos_twist, sin_twist = phase_tables(trains, bunch_dev, bunch_total)
    twist_re = first_re * cos_twist + first_im * sin_twist
    twist_im = first_im * cos_twist - first_re * sin_twist
    cos_local, sin_local = phase_tables(bunch_dev, bunch_dev, bunch_dev)
    spec_re = contract("qj,nckj->ncqk", cos_local, twist_re) + contract(
        "qj,nckj->ncqk", sin_local, twist_im
    )
    spec_im = contract("qj,nckj->ncqk", cos_local, twist_im) - contract(
        "qj,nckj->ncqk", sin_local, twist_re
    )
    return (
        spec_re.reshape(item_count, column_count, bunch_total),
        spec_im.reshape(item_count, column_count, bunch_total),
    )


def inverse(summed_re, summed_im):
    column_count, bunch_total = summed_re.shape
    trains = lax.axis_size("train")
    bunch_dev = bunch_total // trains
    grid_re = summed_re.reshape(column_count, bunch_dev, trains)
    grid_im = summed_im.reshape(column_count, bunch_dev, trains)
    cos_local, sin_local = phase_tables(bunch_dev, bunch_dev, bunch_dev)
    back_re = contract("qj,cqk->ckj", cos_local, grid_re) - contract(
        "qj,cqk->ckj", sin_local, grid_im
    )
    back_im = contract("qj,cqk->ckj", cos_local, grid_im) + contract(
        "qj,cqk->ckj", sin_local, grid_re
    )
    cos_twist, sin_twist = phase_tables(trains, bunch_dev, bunch_total)
    turned_re = back_re * cos_twist - back_im * sin_twist
    turned_im = back_re * sin_twist + back_im * cos_twist
    cos_train, sin_train = phase_tables(trains, trains, trains)
    field = (
        contract("kp,ckj->cpj", cos_train, turned_re)
        - contract("kp,ckj->cpj", sin_train, turned_im)
    ) / bunch_total
    return field.reshape(column_count, bunch_total)


def local(coordinates, slice_index, history, impedance, slice_wake, tunes, detuning):
    particle_count = slice_index.shape[0]
    slice_count = slice_wake.shape[0]
    bunch_dev = history.shape[3]
    turn_total = history.shape[0] + 1
    per_bunch = particle_count // bunch_dev
    bunch_group = math.gcd(bunch_dev, 16)
    group_count = bunch_dev // bunch_group
    group_span = bunch_group * per_bunch
    levels = lax.broadcasted_iota(jnp.int32, (1, 1, slice_count), 2)

    def selector(group_index):
        picked = lax.dynamic_slice_in_dim(slice_index, group_index * group_span, group_span)
        picked = picked.reshape(bunch_group, per_bunch)
        return (picked[:, :, None] == levels).astype(jnp.float32)

    def deposit(group_index, gathered):
        onehot = selector(group_index)
        section = lax.dynamic_slice_in_dim(coordinates, group_index * group_span, group_span, 1)
        transverse = section[0::2].reshape(2, bunch_group, per_bunch)
        sums = contract("gps,cgp->csg", onehot, transverse)
        return lax.dynamic_update_slice_in_dim(
            gathered, sums * (slice_count / per_bunch), group_index * bunch_group, 2
        )

    moments = lax.fori_loop(
        0, group_count, deposit, jnp.zeros((2, slice_count, bunch_dev), jnp.float32)
    )
    series = jnp.concatenate([moments[None], history], 0).reshape(
        turn_total, 2 * slice_count, bunch_dev
    )
    imp_re = impedance[:, 0, :]
    imp_im = impedance[:, 1, :]
    spec_re, spec_im = forward(
        lax.all_to_all(series, "train", split_axis=1, concat_axis=2, tiled=True)
    )
    summed_re = jnp.sum(imp_re[:, None, :] * spec_re - imp_im[:, None, :] * spec_im, axis=0)
    summed_im = jnp.sum(imp_re[:, None, :] * spec_im + imp_im[:, None, :] * spec_re, axis=0)
    field = inverse(summed_re, summed_im)
    home = lax.all_to_all(field, "train", split_axis=1, concat_axis=0, tiled=True).reshape(
        2, slice_count, bunch_dev
    )
    kicks = contract("st,ctb->csb", slice_wake, home)

    def track(group_index, moved):
        onehot = selector(group_index)
        local_kicks = lax.dynamic_slice_in_dim(kicks, group_index * bunch_group, bunch_group, 2)
        pushes = contract("gps,csg->cgp", onehot, local_kicks).reshape(2, group_span)
        section = lax.dynamic_slice_in_dim(coordinates, group_index * group_span, group_span, 1)
        turned = rotate(section, pushes, tunes, detuning)
        return lax.dynamic_update_slice_in_dim(moved, turned, group_index * group_span, 1)

    tracked = lax.fori_loop(0, group_count, track, jnp.zeros_like(coordinates))
    return (tracked, moments)


def solution(mesh):
    return jax.shard_map(
        local,
        mesh=mesh,
        in_specs=(
            P("seed", "train"),
            P(("seed", "train")),
            P("seed", None, None, "train"),
            P(),
            P(),
            P("seed"),
            P("seed"),
        ),
        out_specs=(P("seed", "train"), P("seed", None, "train")),
        check_vma=False,
    )
```

profile of v0, /device:TPU:0, one launch (start us, length us, event | category | flops | bytes accessed | tf_op | source)
XLA Modules:
  0.0 208.2 jit_solution(1865617908062196139)
XLA Ops:
  0.7 37.9 %while.30 = (s32[]{:T(128)}, f32[2,128,128]{1,0,2:T(2,128)S(1)}, f32[4,65536]{1,0:T(4,128)}, s32[65536]{0:T(1024)}, s32[]{:T(128)}, /*index=5*/s32[]{:T(128)}, s32[]{:T(128)}, s32[]{:T(128)}, s32[]{:T(128)}, s32[]{:T(128)}) while((s32[]{:T(128)}, f32[2,128,128]{1,0,2:T(2,128)S(1)}, f32[4,65536]{1,0:T(4,128)}, s32[65536]{0:T(1024)}, ...), condition=%wide.region_1.0_spmd.clone, body=%wide.region_0.0_spmd.clone.sunk | while | flops 26218504 | bytes 639181 | solution.py:108
  3.1 2.4 %fusion.152 = f32[2,128,128]{1,0,2:T(2,128)S(1)} fusion(f32[2,128,128]{1,0,2:T(2,128)S(1)} %get-tuple-element.530, s32[]{:T(128)S(6)} %select_n.184, f32[2,16,512]{2,0,1:T(2,128)S(1)} %bitcast.100, s32[16,512]{1,0:T(8,128)S(1)} %eq.147), kind=kOutput, calls=%fused_computation.7.clone.1 | convolution fusion | flops 26218496 | bytes 114692 | tf_op jit(solution)/shard_map/while/body/eval_jaxpr/gps,cgp->csg/dot_general | solution.py:32
  7.8 2.4 %fusion.152 = f32[2,128,128]{1,0,2:T(2,128)S(1)} fusion(f32[2,128,128]{1,0,2:T(2,128)S(1)} %get-tuple-element.530, s32[]{:T(128)S(6)} %select_n.184, f32[2,16,512]{2,0,1:T(2,128)S(1)} %bitcast.100, s32[16,512]{1,0:T(8,128)S(1)} %eq.147), kind=kOutput, calls=%fused_computation.7.clone.1 | convolution fusion | flops 26218496 | bytes 114692 | tf_op jit(solution)/shard_map/while/body/eval_jaxpr/gps,cgp->csg/dot_general | solution.py:32
  12.5 2.4 %fusion.152 = f32[2,128,128]{1,0,2:T(2,128)S(1)} fusion(f32[2,128,128]{1,0,2:T(2,128)S(1)} %get-tuple-element.530, s32[]{:T(128)S(6)} %select_n.184, f32[2,16,512]{2,0,1:T(2,128)S(1)} %bitcast.100, s32[16,512]{1,0:T(8,128)S(1)} %eq.147), kind=kOutput, calls=%fused_computation.7.clone.1 | convolution fusion | flops 26218496 | bytes 114692 | tf_op jit(solution)/shard_map/while/body/eval_jaxpr/gps,cgp->csg/dot_general | solution.py:32
  17.3 2.4 %fusion.152 = f32[2,128,128]{1,0,2:T(2,128)S(1)} fusion(f32[2,128,128]{1,0,2:T(2,128)S(1)} %get-tuple-element.530, s32[]{:T(128)S(6)} %select_n.184, f32[2,16,512]{2,0,1:T(2,128)S(1)} %bitcast.100, s32[16,512]{1,0:T(8,128)S(1)} %eq.147), kind=kOutput, calls=%fused_computation.7.clone.1 | convolution fusion | flops 26218496 | bytes 114692 | tf_op jit(solution)/shard_map/while/body/eval_jaxpr/gps,cgp->csg/dot_general | solution.py:32
  22.0 2.4 %fusion.152 = f32[2,128,128]{1,0,2:T(2,128)S(1)} fusion(f32[2,128,128]{1,0,2:T(2,128)S(1)} %get-tuple-element.530, s32[]{:T(128)S(6)} %select_n.184, f32[2,16,512]{2,0,1:T(2,128)S(1)} %bitcast.100, s32[16,512]{1,0:T(8,128)S(1)} %eq.147), kind=kOutput, calls=%fused_computation.7.clone.1 | convolution fusion | flops 26218496 | bytes 114692 | tf_op jit(solution)/shard_map/while/body/eval_jaxpr/gps,cgp->csg/dot_general | solution.py:32
  26.7 2.4 %fusion.152 = f32[2,128,128]{1,0,2:T(2,128)S(1)} fusion(f32[2,128,128]{1,0,2:T(2,128)S(1)} %get-tuple-element.530, s32[]{:T(128)S(6)} %select_n.184, f32[2,16,512]{2,0,1:T(2,128)S(1)} %bitcast.100, s32[16,512]{1,0:T(8,128)S(1)} %eq.147), kind=kOutput, calls=%fused_computation.7.clone.1 | convolution fusion | flops 26218496 | bytes 114692 | tf_op jit(solution)/shard_map/while/body/eval_jaxpr/gps,cgp->csg/dot_general | solution.py:32
  31.5 2.4 %fusion.152 = f32[2,128,128]{1,0,2:T(2,128)S(1)} fusion(f32[2,128,128]{1,0,2:T(2,128)S(1)} %get-tuple-element.530, s32[]{:T(128)S(6)} %select_n.184, f32[2,16,512]{2,0,1:T(2,128)S(1)} %bitcast.100, s32[16,512]{1,0:T(8,128)S(1)} %eq.147), kind=kOutput, calls=%fused_computation.7.clone.1 | convolution fusion | flops 26218496 | bytes 114692 | tf_op jit(solution)/shard_map/while/body/eval_jaxpr/gps,cgp->csg/dot_general | solution.py:32
  36.2 2.4 %fusion.152 = f32[2,128,128]{1,0,2:T(2,128)S(1)} fusion(f32[2,128,128]{1,0,2:T(2,128)S(1)} %get-tuple-element.530, s32[]{:T(128)S(6)} %select_n.184, f32[2,16,512]{2,0,1:T(2,128)S(1)} %bitcast.100, s32[16,512]{1,0:T(8,128)S(1)} %eq.147), kind=kOutput, calls=%fused_computation.7.clone.1 | convolution fusion | flops 26218496 | bytes 114692 | tf_op jit(solution)/shard_map/while/body/eval_jaxpr/gps,cgp->csg/dot_general | solution.py:32
  41.0 7.4 %all-to-all-start = ((f32[9,256,128]{2,0,1:T(8,128)}), f32[9,256,128]{2,0,1:T(8,128)S(1)}, u32[]{:S(2)}, u32[]{:S(2)}) async-start(f32[9,256,128]{2,0,1:T(8,128)} %pad_maximum_fusion), calls=%async_computation | async-start | bytes 4194304 | tf_op jit(solution)/shard_map/all_to_all | solution.py:117
  49.8 46.9 %all-to-all-done = f32[9,256,128]{2,0,1:T(8,128)S(1)} async-done(((f32[9,256,128]{2,0,1:T(8,128)}), f32[9,256,128]{2,0,1:T(8,128)S(1)}, u32[]{:S(2)}, u32[]{:S(2)}) %all-to-all-start) | async-done | bytes 1179680 | tf_op jit(solution)/shard_map/all_to_all | solution.py:117
  96.7 1.9 convolution_bitcast_fusion
  98.5 1.9 fusion.13
  109.7 3.6 %all-to-all-start.1 = ((f32[32,8,128]{2,0,1:T(8,128)}), f32[32,8,128]{2,0,1:T(8,128)S(1)}, u32[]{:S(2)}, u32[]{:S(2)}) async-start(f32[32,8,128]{2,0,1:T(8,128)} %copy.34), calls=%async_computation.1 | async-start | bytes 262144 | tf_op jit(solution)/shard_map/all_to_all | solution.py:122
  117.0 3.7 %all-to-all-done.1 = f32[32,8,128]{2,0,1:T(8,128)S(1)} async-done(((f32[32,8,128]{2,0,1:T(8,128)}), f32[32,8,128]{2,0,1:T(8,128)S(1)}, u32[]{:S(2)}, u32[]{:S(2)}) %all-to-all-start.1) | async-done | bytes 131104 | tf_op jit(solution)/shard_map/all_to_all | solution.py:122
  121.2 86.0 %while.31 = (s32[]{:T(128)}, f32[4,65536]{1,0:T(4,128)S(1)}, f32[]{:T(128)}, f32[4,65536]{1,0:T(4,128)}, f32[2,128,128]{1,2,0:T(8,128)S(1)}, /*index=5*/s32[6553...) while((s32[]{:T(128)}, f32[4,65536]{1,0:T(4,128)S(1)}, ...), condition=%wide.region_5.6_spmd.clone, body=%wide.region_4.5_spmd.clone.sunk | while | flops 26509320 | bytes 1458525 | solution.py:135
  122.0 2.9 %fusion.154 = f32[2,16,512]{2,0,1:T(2,128)S(1)} fusion(s32[16,512]{1,0:T(8,128)S(1)} %eq.150, f32[2,128,16]{1,2,0:T(8,128)S(1)} %constant_dynamic-slice_fusion.5), kind=kOutput, calls=%fused_computation.12.clone.1 | convolution fusion | flops 26214400 | bytes 114688 | tf_op jit(solution)/shard_map/while/body/eval_jaxpr/gps,csg->cgp/dot_general | solution.py:32
  125.0 1.9 fusion.156
  127.0 3.0 %multiply_add_fusion.11 = (f32[1,8192]{1,0:T(1,128)S(1)}, f32[1,8192]{1,0:T(1,128)S(1)}, f32[1,8192]{1,0:T(1,128)S(1)}, f32[1,8192]{1,0:T(1,128)S(1)}, f32[1,8192]{1,0:T(1,128)S(1)}) fusion(f32[1,8192]{1,0:T(1,128)S(1)} %get-tuple-element.508, f32[1,8192]{1,0:T(1,128)S(1)} %get-tuple-element.509, f32[4,65536]{1,0:T(4,128)} %get-tuple-element.588, ...), kind=kLoop, calls=%fused_computation.20.clone.1 | loop fusion | flops 98304 | bytes 393236 | tf_op jit(solution)/shard_map/while/body/eval_jaxpr/add | solution.py:19
  130.0 1.8 multiply_add_fusion.12
  132.8 2.9 %fusion.154 = f32[2,16,512]{2,0,1:T(2,128)S(1)} fusion(s32[16,512]{1,0:T(8,128)S(1)} %eq.150, f32[2,128,16]{1,2,0:T(8,128)S(1)} %constant_dynamic-slice_fusion.5), kind=kOutput, calls=%fused_computation.12.clone.1 | convolution fusion | flops 26214400 | bytes 114688 | tf_op jit(solution)/shard_map/while/body/eval_jaxpr/gps,csg->cgp/dot_general | solution.py:32
  135.8 1.9 fusion.156
  137.7 3.0 %multiply_add_fusion.11 = (f32[1,8192]{1,0:T(1,128)S(1)}, f32[1,8192]{1,0:T(1,128)S(1)}, f32[1,8192]{1,0:T(1,128)S(1)}, f32[1,8192]{1,0:T(1,128)S(1)}, f32[1,8192]{1,0:T(1,128)S(1)}) fusion(f32[1,8192]{1,0:T(1,128)S(1)} %get-tuple-element.508, f32[1,8192]{1,0:T(1,128)S(1)} %get-tuple-element.509, f32[4,65536]{1,0:T(4,128)} %get-tuple-element.588, ...), kind=kLoop, calls=%fused_computation.20.clone.1 | loop fusion | flops 98304 | bytes 393236 | tf_op jit(solution)/shard_map/while/body/eval_jaxpr/add | solution.py:19
  140.7 1.8 multiply_add_fusion.12
  143.5 2.9 %fusion.154 = f32[2,16,512]{2,0,1:T(2,128)S(1)} fusion(s32[16,512]{1,0:T(8,128)S(1)} %eq.150, f32[2,128,16]{1,2,0:T(8,128)S(1)} %constant_dynamic-slice_fusion.5), kind=kOutput, calls=%fused_computation.12.clone.1 | convolution fusion | flops 26214400 | bytes 114688 | tf_op jit(solution)/shard_map/while/body/eval_jaxpr/gps,csg->cgp/dot_general | solution.py:32
  146.5 1.9 fusion.156
  148.5 3.0 %multiply_add_fusion.11 = (f32[1,8192]{1,0:T(1,128)S(1)}, f32[1,8192]{1,0:T(1,128)S(1)}, f32[1,8192]{1,0:T(1,128)S(1)}, f32[1,8192]{1,0:T(1,128)S(1)}, f32[1,8192]{1,0:T(1,128)S(1)}) fusion(f32[1,8192]{1,0:T(1,128)S(1)} %get-tuple-element.508, f32[1,8192]{1,0:T(1,128)S(1)} %get-tuple-element.509, f32[4,65536]{1,0:T(4,128)} %get-tuple-element.588, ...), kind=kLoop, calls=%fused_computation.20.clone.1 | loop fusion | flops 98304 | bytes 393236 | tf_op jit(solution)/shard_map/while/body/eval_jaxpr/add | solution.py:19
  151.5 1.8 multiply_add_fusion.12
  154.3 2.9 %fusion.154 = f32[2,16,512]{2,0,1:T(2,128)S(1)} fusion(s32[16,512]{1,0:T(8,128)S(1)} %eq.150, f32[2,128,16]{1,2,0:T(8,128)S(1)} %constant_dynamic-slice_fusion.5), kind=kOutput, calls=%fused_computation.12.clone.1 | convolution fusion | flops 26214400 | bytes 114688 | tf_op jit(solution)/shard_map/while/body/eval_jaxpr/gps,csg->cgp/dot_general | solution.py:32
  157.3 1.9 fusion.156
  159.2 3.0 %multiply_add_fusion.11 = (f32[1,8192]{1,0:T(1,128)S(1)}, f32[1,8192]{1,0:T(1,128)S(1)}, f32[1,8192]{1,0:T(1,128)S(1)}, f32[1,8192]{1,0:T(1,128)S(1)}, f32[1,8192]{1,0:T(1,128)S(1)}) fusion(f32[1,8192]{1,0:T(1,128)S(1)} %get-tuple-element.508, f32[1,8192]{1,0:T(1,128)S(1)} %get-tuple-element.509, f32[4,65536]{1,0:T(4,128)} %get-tuple-element.588, ...), kind=kLoop, calls=%fused_computation.20.clone.1 | loop fusion | flops 98304 | bytes 393236 | tf_op jit(solution)/shard_map/while/body/eval_jaxpr/add | solution.py:19
  162.2 1.8 multiply_add_fusion.12
  165.0 2.9 %fusion.154 = f32[2,16,512]{2,0,1:T(2,128)S(1)} fusion(s32[16,512]{1,0:T(8,128)S(1)} %eq.150, f32[2,128,16]{1,2,0:T(8,128)S(1)} %constant_dynamic-slice_fusion.5), kind=kOutput, calls=%fused_computation.12.clone.1 | convolution fusion | flops 26214400 | bytes 114688 | tf_op jit(solution)/shard_map/while/body/eval_jaxpr/gps,csg->cgp/dot_general | solution.py:32
  168.0 1.9 fusion.156
  170.0 3.0 %multiply_add_fusion.11 = (f32[1,8192]{1,0:T(1,128)S(1)}, f32[1,8192]{1,0:T(1,128)S(1)}, f32[1,8192]{1,0:T(1,128)S(1)}, f32[1,8192]{1,0:T(1,128)S(1)}, f32[1,8192]{1,0:T(1,128)S(1)}) fusion(f32[1,8192]{1,0:T(1,128)S(1)} %get-tuple-element.508, f32[1,8192]{1,0:T(1,128)S(1)} %get-tuple-element.509, f32[4,65536]{1,0:T(4,128)} %get-tuple-element.588, ...), kind=kLoop, calls=%fused_computation.20.clone.1 | loop fusion | flops 98304 | bytes 393236 | tf_op jit(solution)/shard_map/while/body/eval_jaxpr/add | solution.py:19
  172.9 1.8 multiply_add_fusion.12
  175.8 2.9 %fusion.154 = f32[2,16,512]{2,0,1:T(2,128)S(1)} fusion(s32[16,512]{1,0:T(8,128)S(1)} %eq.150, f32[2,128,16]{1,2,0:T(8,128)S(1)} %constant_dynamic-slice_fusion.5), kind=kOutput, calls=%fused_computation.12.clone.1 | convolution fusion | flops 26214400 | bytes 114688 | tf_op jit(solution)/shard_map/while/body/eval_jaxpr/gps,csg->cgp/dot_general | solution.py:32
  178.8 1.9 fusion.156
  180.7 3.0 %multiply_add_fusion.11 = (f32[1,8192]{1,0:T(1,128)S(1)}, f32[1,8192]{1,0:T(1,128)S(1)}, f32[1,8192]{1,0:T(1,128)S(1)}, f32[1,8192]{1,0:T(1,128)S(1)}, f32[1,8192]{1,0:T(1,128)S(1)}) fusion(f32[1,8192]{1,0:T(1,128)S(1)} %get-tuple-element.508, f32[1,8192]{1,0:T(1,128)S(1)} %get-tuple-element.509, f32[4,65536]{1,0:T(4,128)} %get-tuple-element.588, ...), kind=kLoop, calls=%fused_computation.20.clone.1 | loop fusion | flops 98304 | bytes 393236 | tf_op jit(solution)/shard_map/while/body/eval_jaxpr/add | solution.py:19
  183.7 1.8 multiply_add_fusion.12
  186.5 2.9 %fusion.154 = f32[2,16,512]{2,0,1:T(2,128)S(1)} fusion(s32[16,512]{1,0:T(8,128)S(1)} %eq.150, f32[2,128,16]{1,2,0:T(8,128)S(1)} %constant_dynamic-slice_fusion.5), kind=kOutput, calls=%fused_computation.12.clone.1 | convolution fusion | flops 26214400 | bytes 114688 | tf_op jit(solution)/shard_map/while/body/eval_jaxpr/gps,csg->cgp/dot_general | solution.py:32
  189.5 1.9 fusion.156
  191.5 3.0 %multiply_add_fusion.11 = (f32[1,8192]{1,0:T(1,128)S(1)}, f32[1,8192]{1,0:T(1,128)S(1)}, f32[1,8192]{1,0:T(1,128)S(1)}, f32[1,8192]{1,0:T(1,128)S(1)}, f32[1,8192]{1,0:T(1,128)S(1)}) fusion(f32[1,8192]{1,0:T(1,128)S(1)} %get-tuple-element.508, f32[1,8192]{1,0:T(1,128)S(1)} %get-tuple-element.509, f32[4,65536]{1,0:T(4,128)} %get-tuple-element.588, ...), kind=kLoop, calls=%fused_computation.20.clone.1 | loop fusion | flops 98304 | bytes 393236 | tf_op jit(solution)/shard_map/while/body/eval_jaxpr/add | solution.py:19
  194.4 1.8 multiply_add_fusion.12
  197.3 2.9 %fusion.154 = f32[2,16,512]{2,0,1:T(2,128)S(1)} fusion(s32[16,512]{1,0:T(8,128)S(1)} %eq.150, f32[2,128,16]{1,2,0:T(8,128)S(1)} %constant_dynamic-slice_fusion.5), kind=kOutput, calls=%fused_computation.12.clone.1 | convolution fusion | flops 26214400 | bytes 114688 | tf_op jit(solution)/shard_map/while/body/eval_jaxpr/gps,csg->cgp/dot_general | solution.py:32
  200.2 1.9 fusion.156
  202.2 3.0 %multiply_add_fusion.11 = (f32[1,8192]{1,0:T(1,128)S(1)}, f32[1,8192]{1,0:T(1,128)S(1)}, f32[1,8192]{1,0:T(1,128)S(1)}, f32[1,8192]{1,0:T(1,128)S(1)}, f32[1,8192]{1,0:T(1,128)S(1)}) fusion(f32[1,8192]{1,0:T(1,128)S(1)} %get-tuple-element.508, f32[1,8192]{1,0:T(1,128)S(1)} %get-tuple-element.509, f32[4,65536]{1,0:T(4,128)} %get-tuple-element.588, ...), kind=kLoop, calls=%fused_computation.20.clone.1 | loop fusion | flops 98304 | bytes 393236 | tf_op jit(solution)/shard_map/while/body/eval_jaxpr/add | solution.py:19
  205.2 1.8 multiply_add_fusion.12
  (111 shorter events, 41.8 us)
Async XLA Ops:
  0.6 120.0 %copy-start = (f32[128,128]{1,0:T(8,128)S(1)}, f32[128,128]{1,0:T(8,128)}, u32[]{:S(2)}) copy-start(f32[128,128]{1,0:T(8,128)} %param.15) | copy-start | bytes 196612
  0.7 38.1 %copy-start.1 = (f32[8,2,128,128]{3,2,1,0:T(8,128)S(1)}, f32[8,2,128,128]{3,2,1,0:T(8,128)}, u32[]{:S(2)}) copy-start(f32[8,2,128,128]{3,2,1,0:T(8,128)} %param.13) | copy-start | bytes 3145732
  38.8 2.2 %copy-start.3 = (f32[2,128,128]{2,1,0:T(8,128)}, f32[2,128,128]{2,1,0:T(8,128)S(1)}, u32[]{:S(2)}) copy-start(f32[2,128,128]{2,1,0:T(8,128)S(1)} %copy.27) | copy-start | bytes 393220
  41.0 7.4 %copy-start.4 = (f32[9,2,1024]{2,1,0:T(2,128)S(1)}, f32[9,2,1024]{2,1,0:T(2,128)}, u32[]{:S(2)}) copy-start(f32[9,2,1024]{2,1,0:T(2,128)} %param.14) | copy-start | bytes 221188
  41.0 55.7 %all-to-all-start = ((f32[9,256,128]{2,0,1:T(8,128)}), f32[9,256,128]{2,0,1:T(8,128)S(1)}, u32[]{:S(2)}, u32[]{:S(2)}) async-start(f32[9,256,128]{2,0,1:T(8,128)} %pad_maximum_fusion), calls=%async_computation | async-start | bytes 4194304 | tf_op jit(solution)/shard_map/all_to_all | solution.py:117
  107.1 6.2 %copy-start.5 = (f32[2]{0:T(128)S(1)}, f32[2]{0:T(128)}, u32[]{:S(2)}) copy-start(f32[2]{0:T(128)} %param.16) | copy-start | bytes 28
  107.2 8.0 %copy-start.6 = (f32[2]{0:T(128)S(1)}, f32[2]{0:T(128)}, u32[]{:S(2)}) copy-start(f32[2]{0:T(128)} %param.17) | copy-start | bytes 28
  109.7 11.0 %all-to-all-start.1 = ((f32[32,8,128]{2,0,1:T(8,128)}), f32[32,8,128]{2,0,1:T(8,128)S(1)}, u32[]{:S(2)}, u32[]{:S(2)}) async-start(f32[32,8,128]{2,0,1:T(8,128)} %copy.34), calls=%async_computation.1 | async-start | bytes 262144 | tf_op jit(solution)/shard_map/all_to_all | solution.py:122
  207.2 1.0 copy-start.2
where the time goes:
time: 210 us; the launch traced here: 208 us
  other arithmetic  57 us (27%)
  matrix products  55.4 us (26%)
  waiting for transfers between devices  50.5 us (24%)
  local copies, waits for them, and re-layouts  30 us (14%)
  starting transfers between devices  11.1 us (5%)
  between operations  3.32 us (2%)
    dot_general x29, matrix products, contract(): return jnp.einsum(form, table, values, precision=lax.Precision.HIGHEST)  55.4 us
    all_to_all x1, waiting for transfers between devices, local(): lax.all_to_all(series, 'train', split_axis=1, concat_axis=2, tiled=True)  46.9 us
    add x16, other arithmetic, rotate(): result.append(cosine * position + sine * slope)  38.6 us
    cos x8, other arithmetic, rotate(): cosine = jnp.cos(phase)  15.5 us
    dynamic_slice x16, local copies, waits for them, and re-layouts, selector(): lax.dynamic_slice_in_dim(slice_index, group_index * group_span, group_span)  12.3 us
    all_to_all x1, starting transfers between devices, local(): lax.all_to_all(series, 'train', split_axis=1, concat_axis=2, tiled=True)  7.44 us
    dynamic_slice x8, local copies, waits for them, and re-layouts, deposit(): lax.dynamic_slice_in_dim(coordinates, group_index * group_span, group_spa...  7.43 us
    slice x8, local copies, waits for them, and re-layouts, deposit(): transverse = section[0::2].reshape(2, bunch_group, per_bunch)  4.52 us
  transfers between devices with their start and end apart: 2, of which 2 were waited for; matrix products, arithmetic and copies ran while one was open for 1% of the time, Pallas kernels for 0%

commit v1 on v0

--- a/solution.py
+++ b/solution.py
@@ -114,7 +114,12 @@
     imp_re = impedance[:, 0, :]
     imp_im = impedance[:, 1, :]
     spec_re, spec_im = forward(
-        lax.all_to_all(series, "train", split_axis=1, concat_axis=2, tiled=True)
+        jnp.concatenate(
+            lax.all_to_all(
+                jnp.stack(jnp.split(series, lax.axis_size("train"), axis=1)), "train", 0, 0
+            ),
+            axis=2,
+        )
     )
     summed_re = jnp.sum(imp_re[:, None, :] * spec_re - imp_im[:, None, :] * spec_im, axis=0)
     summed_im = jnp.sum(imp_re[:, None, :] * spec_im + imp_im[:, None, :] * spec_re, axis=0)

time: 210 us -> 194 us (0.924)
  waiting for transfers between devices: 50.5 us -> 30.9 us
  other arithmetic: 57 us -> 60.8 us
    all_to_all x1, waiting for transfers between devices: 46.9 us -> 27.2 us  [local(): lax.all_to_all(jnp.stack(jnp.split(series, lax.axis_size('train'), axis=1...]
    unnamed x0 -> x7, other arithmetic: none -> 4.68 us
where the time goes in v1:
time: 194 us; the launch traced here: 192 us
  other arithmetic  60.8 us (31%)
  matrix products  55.4 us (29%)
  waiting for transfers between devices  30.9 us (16%)
  local copies, waits for them, and re-layouts  29.3 us (15%)
  starting transfers between devices  11.1 us (6%)
  between operations  3.32 us (2%)
    dot_general x29, matrix products, contract(): return jnp.einsum(form, table, values, precision=lax.Precision.HIGHEST)  55.4 us
    add x16, other arithmetic, rotate(): result.append(cosine * position + sine * slope)  38.6 us
    all_to_all x1, waiting for transfers between devices, local(): lax.all_to_all(jnp.stack(jnp.split(series, lax.axis_size('train'), axis=1...  27.2 us
    cos x8, other arithmetic, rotate(): cosine = jnp.cos(phase)  15.5 us
    dynamic_slice x16, local copies, waits for them, and re-layouts, selector(): lax.dynamic_slice_in_dim(slice_index, group_index * group_span, group_span)  12.3 us
    all_to_all x1, starting transfers between devices, local(): lax.all_to_all(jnp.stack(jnp.split(series, lax.axis_size('train'), axis=1...  7.44 us
    dynamic_slice x8, local copies, waits for them, and re-layouts, deposit(): lax.dynamic_slice_in_dim(coordinates, group_index * group_span, group_spa...  7.43 us
    unnamed x7, other arithmetic  4.68 us
  transfers between devices with their start and end apart: 2, of which 2 were waited for; matrix products, arithmetic and copies ran while one was open for 1% of the time, Pallas kernels for 0%

profile of v1, /device:TPU:0, one launch (start us, length us, event | category | flops | bytes accessed | tf_op | source)
XLA Modules:
  0.0 191.6 jit_solution(5758421950268604145)
XLA Ops:
  0.7 37.9 %while.30 = (s32[]{:T(128)}, f32[2,128,128]{1,0,2:T(2,128)S(1)}, f32[4,65536]{1,0:T(4,128)}, s32[65536]{0:T(1024)}, s32[]{:T(128)}, /*index=5*/s32[]{:T(128)}, s32[]{:T(128)}, s32[]{:T(128)}, s32[]{:T(128)}, s32[]{:T(128)}) while((s32[]{:T(128)}, f32[2,128,128]{1,0,2:T(2,128)S(1)}, f32[4,65536]{1,0:T(4,128)}, s32[65536]{0:T(1024)}, ...), condition=%wide.region_1.0_spmd.clone, body=%wide.region_0.0_spmd.clone.sunk | while | flops 26218504 | bytes 639181 | solution.py:108
  3.1 2.4 %fusion.175 = f32[2,128,128]{1,0,2:T(2,128)S(1)} fusion(f32[2,128,128]{1,0,2:T(2,128)S(1)} %get-tuple-element.530, s32[]{:T(128)S(6)} %select_n.184, f32[2,16,512]{2,0,1:T(2,128)S(1)} %bitcast.144, s32[16,512]{1,0:T(8,128)S(1)} %eq.147), kind=kOutput, calls=%fused_computation.7.clone.1 | convolution fusion | flops 26218496 | bytes 114692 | tf_op jit(solution)/shard_map/while/body/eval_jaxpr/gps,cgp->csg/dot_general | solution.py:32
  7.8 2.4 %fusion.175 = f32[2,128,128]{1,0,2:T(2,128)S(1)} fusion(f32[2,128,128]{1,0,2:T(2,128)S(1)} %get-tuple-element.530, s32[]{:T(128)S(6)} %select_n.184, f32[2,16,512]{2,0,1:T(2,128)S(1)} %bitcast.144, s32[16,512]{1,0:T(8,128)S(1)} %eq.147), kind=kOutput, calls=%fused_computation.7.clone.1 | convolution fusion | flops 26218496 | bytes 114692 | tf_op jit(solution)/shard_map/while/body/eval_jaxpr/gps,cgp->csg/dot_general | solution.py:32
  12.5 2.4 %fusion.175 = f32[2,128,128]{1,0,2:T(2,128)S(1)} fusion(f32[2,128,128]{1,0,2:T(2,128)S(1)} %get-tuple-element.530, s32[]{:T(128)S(6)} %select_n.184, f32[2,16,512]{2,0,1:T(2,128)S(1)} %bitcast.144, s32[16,512]{1,0:T(8,128)S(1)} %eq.147), kind=kOutput, calls=%fused_computation.7.clone.1 | convolution fusion | flops 26218496 | bytes 114692 | tf_op jit(solution)/shard_map/while/body/eval_jaxpr/gps,cgp->csg/dot_general | solution.py:32
  17.3 2.4 %fusion.175 = f32[2,128,128]{1,0,2:T(2,128)S(1)} fusion(f32[2,128,128]{1,0,2:T(2,128)S(1)} %get-tuple-element.530, s32[]{:T(128)S(6)} %select_n.184, f32[2,16,512]{2,0,1:T(2,128)S(1)} %bitcast.144, s32[16,512]{1,0:T(8,128)S(1)} %eq.147), kind=kOutput, calls=%fused_computation.7.clone.1 | convolution fusion | flops 26218496 | bytes 114692 | tf_op jit(solution)/shard_map/while/body/eval_jaxpr/gps,cgp->csg/dot_general | solution.py:32
  22.0 2.4 %fusion.175 = f32[2,128,128]{1,0,2:T(2,128)S(1)} fusion(f32[2,128,128]{1,0,2:T(2,128)S(1)} %get-tuple-element.530, s32[]{:T(128)S(6)} %select_n.184, f32[2,16,512]{2,0,1:T(2,128)S(1)} %bitcast.144, s32[16,512]{1,0:T(8,128)S(1)} %eq.147), kind=kOutput, calls=%fused_computation.7.clone.1 | convolution fusion | flops 26218496 | bytes 114692 | tf_op jit(solution)/shard_map/while/body/eval_jaxpr/gps,cgp->csg/dot_general | solution.py:32
  26.7 2.4 %fusion.175 = f32[2,128,128]{1,0,2:T(2,128)S(1)} fusion(f32[2,128,128]{1,0,2:T(2,128)S(1)} %get-tuple-element.530, s32[]{:T(128)S(6)} %select_n.184, f32[2,16,512]{2,0,1:T(2,128)S(1)} %bitcast.144, s32[16,512]{1,0:T(8,128)S(1)} %eq.147), kind=kOutput, calls=%fused_computation.7.clone.1 | convolution fusion | flops 26218496 | bytes 114692 | tf_op jit(solution)/shard_map/while/body/eval_jaxpr/gps,cgp->csg/dot_general | solution.py:32
  31.5 2.4 %fusion.175 = f32[2,128,128]{1,0,2:T(2,128)S(1)} fusion(f32[2,128,128]{1,0,2:T(2,128)S(1)} %get-tuple-element.530, s32[]{:T(128)S(6)} %select_n.184, f32[2,16,512]{2,0,1:T(2,128)S(1)} %bitcast.144, s32[16,512]{1,0:T(8,128)S(1)} %eq.147), kind=kOutput, calls=%fused_computation.7.clone.1 | convolution fusion | flops 26218496 | bytes 114692 | tf_op jit(solution)/shard_map/while/body/eval_jaxpr/gps,cgp->csg/dot_general | solution.py:32
  36.2 2.4 %fusion.175 = f32[2,128,128]{1,0,2:T(2,128)S(1)} fusion(f32[2,128,128]{1,0,2:T(2,128)S(1)} %get-tuple-element.530, s32[]{:T(128)S(6)} %select_n.184, f32[2,16,512]{2,0,1:T(2,128)S(1)} %bitcast.144, s32[16,512]{1,0:T(8,128)S(1)} %eq.147), kind=kOutput, calls=%fused_computation.7.clone.1 | convolution fusion | flops 26218496 | bytes 114692 | tf_op jit(solution)/shard_map/while/body/eval_jaxpr/gps,cgp->csg/dot_general | solution.py:32
  44.1 7.4 %all-to-all-start = ((f32[8,9,32,128]{3,2,1,0:T(8,128)}), f32[8,9,32,128]{3,2,1,0:T(8,128)S(1)}, u32[]{:S(2)}, u32[]{:S(2)}) async-start(f32[8,9,32,128]{3,2,1,0:T(8,128)} %fusion.46), calls=%async_computation | async-start | bytes 2359296 | tf_op jit(solution)/shard_map/all_to_all | solution.py:118
  52.9 27.2 %all-to-all-done = f32[8,9,32,128]{3,2,1,0:T(8,128)S(1)} async-done(((f32[8,9,32,128]{3,2,1,0:T(8,128)}), f32[8,9,32,128]{3,2,1,0:T(8,128)S(1)}, u32[]{:S(2)}, u32[]{:S(2)}) %all-to-all-start) | async-done | bytes 1179680 | tf_op jit(solution)/shard_map/all_to_all | solution.py:118
  80.1 1.9 convolution_bitcast_fusion
  82.0 1.9 fusion.13
  93.2 3.6 %all-to-all-start.1 = ((f32[32,8,128]{2,0,1:T(8,128)}), f32[32,8,128]{2,0,1:T(8,128)S(1)}, u32[]{:S(2)}, u32[]{:S(2)}) async-start(f32[32,8,128]{2,0,1:T(8,128)} %copy.45), calls=%async_computation.1 | async-start | bytes 262144 | tf_op jit(solution)/shard_map/all_to_all | solution.py:127
  100.5 3.7 %all-to-all-done.1 = f32[32,8,128]{2,0,1:T(8,128)S(1)} async-done(((f32[32,8,128]{2,0,1:T(8,128)}), f32[32,8,128]{2,0,1:T(8,128)S(1)}, u32[]{:S(2)}, u32[]{:S(2)}) %all-to-all-start.1) | async-done | bytes 131104 | tf_op jit(solution)/shard_map/all_to_all | solution.py:127
  104.7 86.0 %while.31 = (s32[]{:T(128)}, f32[4,65536]{1,0:T(4,128)S(1)}, f32[]{:T(128)}, f32[4,65536]{1,0:T(4,128)}, f32[2,128,128]{1,2,0:T(8,128)S(1)}, /*index=5*/s32[6553...) while((s32[]{:T(128)}, f32[4,65536]{1,0:T(4,128)S(1)}, ...), condition=%wide.region_5.6_spmd.clone, body=%wide.region_4.5_spmd.clone.sunk | while | flops 26509320 | bytes 1458525 | solution.py:140
  105.5 2.9 %fusion.177 = f32[2,16,512]{2,0,1:T(2,128)S(1)} fusion(s32[16,512]{1,0:T(8,128)S(1)} %eq.150, f32[2,128,16]{1,2,0:T(8,128)S(1)} %constant_dynamic-slice_fusion.5), kind=kOutput, calls=%fused_computation.12.clone.1 | convolution fusion | flops 26214400 | bytes 114688 | tf_op jit(solution)/shard_map/while/body/eval_jaxpr/gps,csg->cgp/dot_general | solution.py:32
  108.5 1.9 %fusion.179 = (f32[1,8192]{1,0:T(1,128)S(1)}, f32[1,8192]{1,0:T(1,128)S(1)}, f32[1,8192]{1,0:T(1,128)S(1)}) fusion(f32[]{:T(128)} %get-tuple-element.591, f32[4,65536]{1,0:T(4,128)} %get-tuple-element.588, s32[]{:T(128)S(6)} %select_n.186, f32[]{:T(128)} %get-tuple-element.587, f32[1,8192]{1,0:T(1,128)S(1)} %bitcast.143, s32[]{:T(128)S(6)} %add.419), kind=kLoop, calls=%fused_computation.194.clone.1 | loop fusion | flops 49152 | bytes 196624 | tf_op jit(solution)/shard_map/while/body/eval_jaxpr/cos | solution.py:17
  110.4 3.0 %multiply_add_fusion.11 = (f32[1,8192]{1,0:T(1,128)S(1)}, f32[1,8192]{1,0:T(1,128)S(1)}, f32[1,8192]{1,0:T(1,128)S(1)}, f32[1,8192]{1,0:T(1,128)S(1)}, f32[1,8192]{1,0:T(1,128)S(1)}) fusion(f32[1,8192]{1,0:T(1,128)S(1)} %get-tuple-element.508, f32[1,8192]{1,0:T(1,128)S(1)} %get-tuple-element.509, f32[4,65536]{1,0:T(4,128)} %get-tuple-element.588, ...), kind=kLoop, calls=%fused_computation.20.clone.1 | loop fusion | flops 98304 | bytes 393236 | tf_op jit(solution)/shard_map/while/body/eval_jaxpr/add | solution.py:19
  113.4 1.8 multiply_add_fusion.12
  116.2 2.9 %fusion.177 = f32[2,16,512]{2,0,1:T(2,128)S(1)} fusion(s32[16,512]{1,0:T(8,128)S(1)} %eq.150, f32[2,128,16]{1,2,0:T(8,128)S(1)} %constant_dynamic-slice_fusion.5), kind=kOutput, calls=%fused_computation.12.clone.1 | convolution fusion | flops 26214400 | bytes 114688 | tf_op jit(solution)/shard_map/while/body/eval_jaxpr/gps,csg->cgp/dot_general | solution.py:32
  119.2 1.9 %fusion.179 = (f32[1,8192]{1,0:T(1,128)S(1)}, f32[1,8192]{1,0:T(1,128)S(1)}, f32[1,8192]{1,0:T(1,128)S(1)}) fusion(f32[]{:T(128)} %get-tuple-element.591, f32[4,65536]{1,0:T(4,128)} %get-tuple-element.588, s32[]{:T(128)S(6)} %select_n.186, f32[]{:T(128)} %get-tuple-element.587, f32[1,8192]{1,0:T(1,128)S(1)} %bitcast.143, s32[]{:T(128)S(6)} %add.419), kind=kLoop, calls=%fused_computation.194.clone.1 | loop fusion | flops 49152 | bytes 196624 | tf_op jit(solution)/shard_map/while/body/eval_jaxpr/cos | solution.py:17
  121.2 3.0 %multiply_add_fusion.11 = (f32[1,8192]{1,0:T(1,128)S(1)}, f32[1,8192]{1,0:T(1,128)S(1)}, f32[1,8192]{1,0:T(1,128)S(1)}, f32[1,8192]{1,0:T(1,128)S(1)}, f32[1,8192]{1,0:T(1,128)S(1)}) fusion(f32[1,8192]{1,0:T(1,128)S(1)} %get-tuple-element.508, f32[1,8192]{1,0:T(1,128)S(1)} %get-tuple-element.509, f32[4,65536]{1,0:T(4,128)} %get-tuple-element.588, ...), kind=kLoop, calls=%fused_computation.20.clone.1 | loop fusion | flops 98304 | bytes 393236 | tf_op jit(solution)/shard_map/while/body/eval_jaxpr/add | solution.py:19
  124.2 1.8 multiply_add_fusion.12
  127.0 2.9 %fusion.177 = f32[2,16,512]{2,0,1:T(2,128)S(1)} fusion(s32[16,512]{1,0:T(8,128)S(1)} %eq.150, f32[2,128,16]{1,2,0:T(8,128)S(1)} %constant_dynamic-slice_fusion.5), kind=kOutput, calls=%fused_computation.12.clone.1 | convolution fusion | flops 26214400 | bytes 114688 | tf_op jit(solution)/shard_map/while/body/eval_jaxpr/gps,csg->cgp/dot_general | solution.py:32
  130.0 1.9 %fusion.179 = (f32[1,8192]{1,0:T(1,128)S(1)}, f32[1,8192]{1,0:T(1,128)S(1)}, f32[1,8192]{1,0:T(1,128)S(1)}) fusion(f32[]{:T(128)} %get-tuple-element.591, f32[4,65536]{1,0:T(4,128)} %get-tuple-element.588, s32[]{:T(128)S(6)} %select_n.186, f32[]{:T(128)} %get-tuple-element.587, f32[1,8192]{1,0:T(1,128)S(1)} %bitcast.143, s32[]{:T(128)S(6)} %add.419), kind=kLoop, calls=%fused_computation.194.clone.1 | loop fusion | flops 49152 | bytes 196624 | tf_op jit(solution)/shard_map/while/body/eval_jaxpr/cos | solution.py:17
  131.9 3.0 %multiply_add_fusion.11 = (f32[1,8192]{1,0:T(1,128)S(1)}, f32[1,8192]{1,0:T(1,128)S(1)}, f32[1,8192]{1,0:T(1,128)S(1)}, f32[1,8192]{1,0:T(1,128)S(1)}, f32[1,8192]{1,0:T(1,128)S(1)}) fusion(f32[1,8192]{1,0:T(1,128)S(1)} %get-tuple-element.508, f32[1,8192]{1,0:T(1,128)S(1)} %get-tuple-element.509, f32[4,65536]{1,0:T(4,128)} %get-tuple-element.588, ...), kind=kLoop, calls=%fused_computation.20.clone.1 | loop fusion | flops 98304 | bytes 393236 | tf_op jit(solution)/shard_map/while/body/eval_jaxpr/add | solution.py:19
  134.9 1.8 multiply_add_fusion.12
  137.7 2.9 %fusion.177 = f32[2,16,512]{2,0,1:T(2,128)S(1)} fusion(s32[16,512]{1,0:T(8,128)S(1)} %eq.150, f32[2,128,16]{1,2,0:T(8,128)S(1)} %constant_dynamic-slice_fusion.5), kind=kOutput, calls=%fused_computation.12.clone.1 | convolution fusion | flops 26214400 | bytes 114688 | tf_op jit(solution)/shard_map/while/body/eval_jaxpr/gps,csg->cgp/dot_general | solution.py:32
  140.7 1.9 %fusion.179 = (f32[1,8192]{1,0:T(1,128)S(1)}, f32[1,8192]{1,0:T(1,128)S(1)}, f32[1,8192]{1,0:T(1,128)S(1)}) fusion(f32[]{:T(128)} %get-tuple-element.591, f32[4,65536]{1,0:T(4,128)} %get-tuple-element.588, s32[]{:T(128)S(6)} %select_n.186, f32[]{:T(128)} %get-tuple-element.587, f32[1,8192]{1,0:T(1,128)S(1)} %bitcast.143, s32[]{:T(128)S(6)} %add.419), kind=kLoop, calls=%fused_computation.194.clone.1 | loop fusion | flops 49152 | bytes 196624 | tf_op jit(solution)/shard_map/while/body/eval_jaxpr/cos | solution.py:17
  142.7 3.0 %multiply_add_fusion.11 = (f32[1,8192]{1,0:T(1,128)S(1)}, f32[1,8192]{1,0:T(1,128)S(1)}, f32[1,8192]{1,0:T(1,128)S(1)}, f32[1,8192]{1,0:T(1,128)S(1)}, f32[1,8192]{1,0:T(1,128)S(1)}) fusion(f32[1,8192]{1,0:T(1,128)S(1)} %get-tuple-element.508, f32[1,8192]{1,0:T(1,128)S(1)} %get-tuple-element.509, f32[4,65536]{1,0:T(4,128)} %get-tuple-element.588, ...), kind=kLoop, calls=%fused_computation.20.clone.1 | loop fusion | flops 98304 | bytes 393236 | tf_op jit(solution)/shard_map/while/body/eval_jaxpr/add | solution.py:19
  145.7 1.8 multiply_add_fusion.12
  148.5 2.9 %fusion.177 = f32[2,16,512]{2,0,1:T(2,128)S(1)} fusion(s32[16,512]{1,0:T(8,128)S(1)} %eq.150, f32[2,128,16]{1,2,0:T(8,128)S(1)} %constant_dynamic-slice_fusion.5), kind=kOutput, calls=%fused_computation.12.clone.1 | convolution fusion | flops 26214400 | bytes 114688 | tf_op jit(solution)/shard_map/while/body/eval_jaxpr/gps,csg->cgp/dot_general | solution.py:32
  151.5 1.9 %fusion.179 = (f32[1,8192]{1,0:T(1,128)S(1)}, f32[1,8192]{1,0:T(1,128)S(1)}, f32[1,8192]{1,0:T(1,128)S(1)}) fusion(f32[]{:T(128)} %get-tuple-element.591, f32[4,65536]{1,0:T(4,128)} %get-tuple-element.588, s32[]{:T(128)S(6)} %select_n.186, f32[]{:T(128)} %get-tuple-element.587, f32[1,8192]{1,0:T(1,128)S(1)} %bitcast.143, s32[]{:T(128)S(6)} %add.419), kind=kLoop, calls=%fused_computation.194.clone.1 | loop fusion | flops 49152 | bytes 196624 | tf_op jit(solution)/shard_map/while/body/eval_jaxpr/cos | solution.py:17
  153.4 3.0 %multiply_add_fusion.11 = (f32[1,8192]{1,0:T(1,128)S(1)}, f32[1,8192]{1,0:T(1,128)S(1)}, f32[1,8192]{1,0:T(1,128)S(1)}, f32[1,8192]{1,0:T(1,128)S(1)}, f32[1,8192]{1,0:T(1,128)S(1)}) fusion(f32[1,8192]{1,0:T(1,128)S(1)} %get-tuple-element.508, f32[1,8192]{1,0:T(1,128)S(1)} %get-tuple-element.509, f32[4,65536]{1,0:T(4,128)} %get-tuple-element.588, ...), kind=kLoop, calls=%fused_computation.20.clone.1 | loop fusion | flops 98304 | bytes 393236 | tf_op jit(solution)/shard_map/while/body/eval_jaxpr/add | solution.py:19
  156.4 1.8 multiply_add_fusion.12
  159.2 2.9 %fusion.177 = f32[2,16,512]{2,0,1:T(2,128)S(1)} fusion(s32[16,512]{1,0:T(8,128)S(1)} %eq.150, f32[2,128,16]{1,2,0:T(8,128)S(1)} %constant_dynamic-slice_fusion.5), kind=kOutput, calls=%fused_computation.12.clone.1 | convolution fusion | flops 26214400 | bytes 114688 | tf_op jit(solution)/shard_map/while/body/eval_jaxpr/gps,csg->cgp/dot_general | solution.py:32
  162.2 1.9 %fusion.179 = (f32[1,8192]{1,0:T(1,128)S(1)}, f32[1,8192]{1,0:T(1,128)S(1)}, f32[1,8192]{1,0:T(1,128)S(1)}) fusion(f32[]{:T(128)} %get-tuple-element.591, f32[4,65536]{1,0:T(4,128)} %get-tuple-element.588, s32[]{:T(128)S(6)} %select_n.186, f32[]{:T(128)} %get-tuple-element.587, f32[1,8192]{1,0:T(1,128)S(1)} %bitcast.143, s32[]{:T(128)S(6)} %add.419), kind=kLoop, calls=%fused_computation.194.clone.1 | loop fusion | flops 49152 | bytes 196624 | tf_op jit(solution)/shard_map/while/body/eval_jaxpr/cos | solution.py:17
  164.2 3.0 %multiply_add_fusion.11 = (f32[1,8192]{1,0:T(1,128)S(1)}, f32[1,8192]{1,0:T(1,128)S(1)}, f32[1,8192]{1,0:T(1,128)S(1)}, f32[1,8192]{1,0:T(1,128)S(1)}, f32[1,8192]{1,0:T(1,128)S(1)}) fusion(f32[1,8192]{1,0:T(1,128)S(1)} %get-tuple-element.508, f32[1,8192]{1,0:T(1,128)S(1)} %get-tuple-element.509, f32[4,65536]{1,0:T(4,128)} %get-tuple-element.588, ...), kind=kLoop, calls=%fused_computation.20.clone.1 | loop fusion | flops 98304 | bytes 393236 | tf_op jit(solution)/shard_map/while/body/eval_jaxpr/add | solution.py:19
  167.2 1.8 multiply_add_fusion.12
  170.0 2.9 %fusion.177 = f32[2,16,512]{2,0,1:T(2,128)S(1)} fusion(s32[16,512]{1,0:T(8,128)S(1)} %eq.150, f32[2,128,16]{1,2,0:T(8,128)S(1)} %constant_dynamic-slice_fusion.5), kind=kOutput, calls=%fused_computation.12.clone.1 | convolution fusion | flops 26214400 | bytes 114688 | tf_op jit(solution)/shard_map/while/body/eval_jaxpr/gps,csg->cgp/dot_general | solution.py:32
  173.0 1.9 %fusion.179 = (f32[1,8192]{1,0:T(1,128)S(1)}, f32[1,8192]{1,0:T(1,128)S(1)}, f32[1,8192]{1,0:T(1,128)S(1)}) fusion(f32[]{:T(128)} %get-tuple-element.591, f32[4,65536]{1,0:T(4,128)} %get-tuple-element.588, s32[]{:T(128)S(6)} %select_n.186, f32[]{:T(128)} %get-tuple-element.587, f32[1,8192]{1,0:T(1,128)S(1)} %bitcast.143, s32[]{:T(128)S(6)} %add.419), kind=kLoop, calls=%fused_computation.194.clone.1 | loop fusion | flops 49152 | bytes 196624 | tf_op jit(solution)/shard_map/while/body/eval_jaxpr/cos | solution.py:17
  174.9 3.0 %multiply_add_fusion.11 = (f32[1,8192]{1,0:T(1,128)S(1)}, f32[1,8192]{1,0:T(1,128)S(1)}, f32[1,8192]{1,0:T(1,128)S(1)}, f32[1,8192]{1,0:T(1,128)S(1)}, f32[1,8192]{1,0:T(1,128)S(1)}) fusion(f32[1,8192]{1,0:T(1,128)S(1)} %get-tuple-element.508, f32[1,8192]{1,0:T(1,128)S(1)} %get-tuple-element.509, f32[4,65536]{1,0:T(4,128)} %get-tuple-element.588, ...), kind=kLoop, calls=%fused_computation.20.clone.1 | loop fusion | flops 98304 | bytes 393236 | tf_op jit(solution)/shard_map/while/body/eval_jaxpr/add | solution.py:19
  177.9 1.8 multiply_add_fusion.12
  180.7 2.9 %fusion.177 = f32[2,16,512]{2,0,1:T(2,128)S(1)} fusion(s32[16,512]{1,0:T(8,128)S(1)} %eq.150, f32[2,128,16]{1,2,0:T(8,128)S(1)} %constant_dynamic-slice_fusion.5), kind=kOutput, calls=%fused_computation.12.clone.1 | convolution fusion | flops 26214400 | bytes 114688 | tf_op jit(solution)/shard_map/while/body/eval_jaxpr/gps,csg->cgp/dot_general | solution.py:32
  183.7 1.9 %fusion.179 = (f32[1,8192]{1,0:T(1,128)S(1)}, f32[1,8192]{1,0:T(1,128)S(1)}, f32[1,8192]{1,0:T(1,128)S(1)}) fusion(f32[]{:T(128)} %get-tuple-element.591, f32[4,65536]{1,0:T(4,128)} %get-tuple-element.588, s32[]{:T(128)S(6)} %select_n.186, f32[]{:T(128)} %get-tuple-element.587, f32[1,8192]{1,0:T(1,128)S(1)} %bitcast.143, s32[]{:T(128)S(6)} %add.419), kind=kLoop, calls=%fused_computation.194.clone.1 | loop fusion | flops 49152 | bytes 196624 | tf_op jit(solution)/shard_map/while/body/eval_jaxpr/cos | solution.py:17
  185.7 3.0 %multiply_add_fusion.11 = (f32[1,8192]{1,0:T(1,128)S(1)}, f32[1,8192]{1,0:T(1,128)S(1)}, f32[1,8192]{1,0:T(1,128)S(1)}, f32[1,8192]{1,0:T(1,128)S(1)}, f32[1,8192]{1,0:T(1,128)S(1)}) fusion(f32[1,8192]{1,0:T(1,128)S(1)} %get-tuple-element.508, f32[1,8192]{1,0:T(1,128)S(1)} %get-tuple-element.509, f32[4,65536]{1,0:T(4,128)} %get-tuple-element.588, ...), kind=kLoop, calls=%fused_computation.20.clone.1 | loop fusion | flops 98304 | bytes 393236 | tf_op jit(solution)/shard_map/while/body/eval_jaxpr/add | solution.py:19
  188.6 1.8 multiply_add_fusion.12
  (117 shorter events, 44.9 us)
Async XLA Ops:
  0.6 103.5 %copy-start = (f32[128,128]{1,0:T(8,128)S(1)}, f32[128,128]{1,0:T(8,128)}, u32[]{:S(2)}) copy-start(f32[128,128]{1,0:T(8,128)} %param.15) | copy-start | bytes 196612
  0.7 38.1 %copy-start.1 = (f32[8,2,128,128]{3,2,1,0:T(8,128)S(1)}, f32[8,2,128,128]{3,2,1,0:T(8,128)}, u32[]{:S(2)}) copy-start(f32[8,2,128,128]{3,2,1,0:T(8,128)} %param.13) | copy-start | bytes 3145732
  38.7 4.7 %copy-start.2 = (f32[2,128,128]{2,1,0:T(8,128)}, f32[2,128,128]{2,1,0:T(8,128)S(1)}, u32[]{:S(2)}) copy-start(f32[2,128,128]{2,1,0:T(8,128)S(1)} %copy.40) | copy-start | bytes 393220
  44.1 7.4 %copy-start.4 = (f32[9,2,1024]{2,1,0:T(2,128)S(1)}, f32[9,2,1024]{2,1,0:T(2,128)}, u32[]{:S(2)}) copy-start(f32[9,2,1024]{2,1,0:T(2,128)} %param.14) | copy-start | bytes 221188
  44.1 36.0 %all-to-all-start = ((f32[8,9,32,128]{3,2,1,0:T(8,128)}), f32[8,9,32,128]{3,2,1,0:T(8,128)S(1)}, u32[]{:S(2)}, u32[]{:S(2)}) async-start(f32[8,9,32,128]{3,2,1,0:T(8,128)} %fusion.46), calls=%async_computation | async-start | bytes 2359296 | tf_op jit(solution)/shard_map/all_to_all | solution.py:118
  90.6 6.2 %copy-start.5 = (f32[2]{0:T(128)S(1)}, f32[2]{0:T(128)}, u32[]{:S(2)}) copy-start(f32[2]{0:T(128)} %param.16) | copy-start | bytes 28
  90.6 8.0 %copy-start.6 = (f32[2]{0:T(128)S(1)}, f32[2]{0:T(128)}, u32[]{:S(2)}) copy-start(f32[2]{0:T(128)} %param.17) | copy-start | bytes 28
  93.2 11.0 %all-to-all-start.1 = ((f32[32,8,128]{2,0,1:T(8,128)}), f32[32,8,128]{2,0,1:T(8,128)S(1)}, u32[]{:S(2)}, u32[]{:S(2)}) async-start(f32[32,8,128]{2,0,1:T(8,128)} %copy.45), calls=%async_computation.1 | async-start | bytes 262144 | tf_op jit(solution)/shard_map/all_to_all | solution.py:127
  190.7 1.0 copy-start.3
